TPU v7x, 32 devices: a whole 2x2x4 slice. The times are simulated.
32 devices in a mesh: chan: 2 (over x), seq: 16 (over z, y, core).
Axes of the slice: x: 2, y: 2, z: 4, core: 2. Of those that a mesh axis runs over, the one named last changes fastest.
Arguments:
- inputs: bfloat16 [3, 2048, 2, 4096], P(None, 'seq', None, 'chan'), may hold values from -6 to 6
- decay_rate: float32 [4096], P('chan'), may hold values from 0.00024414062 to 0.03
- phase: float32 [4096], P('chan'), may hold values from -3.140625 to 3.140625
- keep: float32 [3, 2048], replicated, may hold values from 0.5 to 1
Outputs:
- states: bfloat16 [3, 2048, 2, 4096], P(None, 'seq', None, 'chan')
All inputs are finite; a program needn't handle non-finite values.
Results may differ from a plain program's by a relative error of at most 0.001.
Values sent between devices are 32-bit elements; how exact they have to be, the bound alone decides.
A program may use at most 64 MiB of HBM per device.

v0:
```python
import jax
import jax.numpy as jnp
from jax import lax
from jax.sharding import PartitionSpec as P


def compose(early, late):
    ear, eai, ebr, ebi = early
    lar, lai, lbr, lbi = late
    return (
        lar * ear - lai * eai,
        lar * eai + lai * ear,
        lar * ebr - lai * ebi + lbr,
        lar * ebi + lai * ebr + lbi,
    )


def coefficients(decay_rate, phase):
    magnitude = jnp.exp(-decay_rate)
    gamma = jnp.sqrt(-jnp.expm1(-2.0 * decay_rate))
    return (magnitude * jnp.cos(phase), magnitude * jnp.sin(phase), gamma)


def apply_carry(prod_re, prod_im, state_re, state_im, carry_re, carry_im):
    final_re = state_re + prod_re * carry_re[None] - prod_im * carry_im[None]
    final_im = state_im + prod_re * carry_im[None] + prod_im * carry_re[None]
    return (final_re, final_im)


def shards(inputs, decay_rate, phase, keep):
    lam_re, lam_im, gamma = coefficients(decay_rate, phase)
    batch = inputs.shape[0]
    rows = inputs.shape[1]
    width = lam_re.shape[0]
    me = lax.axis_index("seq")
    offset = me * rows
    factors = jnp.transpose(lax.dynamic_slice_in_dim(keep, offset, rows, 1))
    dec_re = factors[:, :, None] * lam_re[None, None, :]
    dec_im = factors[:, :, None] * lam_im[None, None, :]
    leading = jnp.transpose(inputs, (1, 2, 0, 3))
    drive_re = leading[:, 0].astype(jnp.float32) * gamma[None, None, :]
    drive_im = leading[:, 1].astype(jnp.float32) * gamma[None, None, :]
    items = (dec_re, dec_im, drive_re, drive_im)
    zeros = jnp.zeros((batch, width), jnp.float32)
    prod_re, prod_im, state_re, state_im = lax.associative_scan(compose, items, axis=0)
    ends = jnp.stack([state_re[-1], state_im[-1]], axis=0)[None]
    gathered = lax.all_gather(ends, "seq", axis=0, tiled=True)
    blocks = lax.axis_size("seq")
    block_keep = jnp.transpose(jnp.prod(keep.reshape(batch, blocks, rows), axis=2))
    span_mag = jnp.exp(-(rows * 1.0) * decay_rate)
    span_re = span_mag * jnp.cos(rows * 1.0 * phase)
    span_im = span_mag * jnp.sin(rows * 1.0 * phase)

    def fold_block(carry, entries):
        index, scale, ended = entries
        carry_re, carry_im = carry
        total_re = scale[:, None] * span_re[None, :]
        total_im = scale[:, None] * span_im[None, :]
        next_re = total_re * carry_re - total_im * carry_im + ended[0]
        next_im = total_re * carry_im + total_im * carry_re + ended[1]
        used = index < me
        return ((jnp.where(used, next_re, carry_re), jnp.where(used, next_im, carry_im)), None)

    (carry_re, carry_im), _ = lax.scan(
        fold_block, (zeros, zeros), (jnp.arange(blocks, dtype=jnp.int32), block_keep, gathered)
    )
    final_re, final_im = apply_carry(prod_re, prod_im, state_re, state_im, carry_re, carry_im)
    joined = jnp.stack([final_re, final_im], axis=1)
    return jnp.transpose(joined, (2, 0, 1, 3)).astype(jnp.bfloat16)


def solution(mesh):
    in_specs = (P(None, "seq", None, "chan"), P("chan"), P("chan"), P())
    out_specs = P(None, "seq", None, "chan")
    return jax.shard_map(shards, mesh=mesh, in_specs=in_specs, out_specs=out_specs, check_vma=False)
```

profile of v0, /device:TPU:0, one launch (start us, length us, event | category | flops | bytes accessed | tf_op | source)
XLA Modules:
  0.0 415.2 jit_solution(14624732573522919704)
XLA Ops:
  12.7 7.8 %slice.517 = f32[63,3,2048]{2,0,1:T(8,128)} slice(f32[128,3,2048]{2,0,1:T(8,128)} %copy-done), slice={[2:128:2], [0:3:1], [0:2048:1]} | slice | bytes 3096576 | tf_op jit(solution)/shard_map/slice | solution.py:45
  20.5 4.4 %slice.422 = f32[63,3,2048]{2,0,1:T(8,128)} slice(f32[128,3,2048]{2,0,1:T(8,128)S(1)} %get-tuple-element.213), slice={[2:128:2], [0:3:1], [0:2048:1]} | slice | bytes 3096576 | tf_op jit(solution)/shard_map/slice | solution.py:45
  24.9 7.8 %slice.521 = f32[63,3,2048]{2,0,1:T(8,128)} slice(f32[128,3,2048]{2,0,1:T(8,128)} %copy-done.2), slice={[2:128:2], [0:3:1], [0:2048:1]} | slice | bytes 3096576 | tf_op jit(solution)/shard_map/slice | solution.py:45
  32.7 7.6 %slice.428 = f32[64,3,2048]{2,0,1:T(8,128)} slice(f32[128,3,2048]{2,0,1:T(8,128)} %copy-done.2), slice={[1:128:2], [0:3:1], [0:2048:1]} | slice | bytes 3145728 | tf_op jit(solution)/shard_map/slice | solution.py:45
  40.3 7.6 %slice.424 = f32[64,3,2048]{2,0,1:T(8,128)} slice(f32[128,3,2048]{2,0,1:T(8,128)} %copy-done.2), slice={[0:127:2], [0:3:1], [0:2048:1]} | slice | bytes 3145728 | tf_op jit(solution)/shard_map/slice | solution.py:45
  47.9 7.8 %slice.549 = f32[63,3,2048]{2,0,1:T(8,128)} slice(f32[128,3,2048]{2,0,1:T(8,128)} %copy-done.1), slice={[2:128:2], [0:3:1], [0:2048:1]} | slice | bytes 3096576 | tf_op jit(solution)/shard_map/slice | solution.py:45
  55.7 7.6 %slice.436 = f32[64,3,2048]{2,0,1:T(8,128)} slice(f32[128,3,2048]{2,0,1:T(8,128)} %copy-done.1), slice={[1:128:2], [0:3:1], [0:2048:1]} | slice | bytes 3145728 | tf_op jit(solution)/shard_map/slice | solution.py:45
  63.3 7.6 %slice.427 = f32[64,3,2048]{2,0,1:T(8,128)} slice(f32[128,3,2048]{2,0,1:T(8,128)} %copy-done.1), slice={[0:127:2], [0:3:1], [0:2048:1]} | slice | bytes 3145728 | tf_op jit(solution)/shard_map/slice | solution.py:45
  70.9 7.6 %slice.431 = f32[64,3,2048]{2,0,1:T(8,128)} slice(f32[128,3,2048]{2,0,1:T(8,128)} %copy-done), slice={[0:127:2], [0:3:1], [0:2048:1]} | slice | bytes 3145728 | tf_op jit(solution)/shard_map/slice | solution.py:45
  78.5 7.6 %slice.425 = f32[64,3,2048]{2,0,1:T(8,128)} slice(f32[128,3,2048]{2,0,1:T(8,128)} %copy-done), slice={[1:128:2], [0:3:1], [0:2048:1]} | slice | bytes 3145728 | tf_op jit(solution)/shard_map/slice | solution.py:45
  86.1 4.2 %slice.430 = f32[64,3,2048]{2,0,1:T(8,128)} slice(f32[128,3,2048]{2,0,1:T(8,128)S(1)} %get-tuple-element.213), slice={[0:127:2], [0:3:1], [0:2048:1]} | slice | bytes 3145728 | tf_op jit(solution)/shard_map/slice | solution.py:45
  90.4 4.3 %slice.423 = f32[64,3,2048]{2,0,1:T(8,128)} slice(f32[128,3,2048]{2,0,1:T(8,128)S(1)} %get-tuple-element.213), slice={[1:128:2], [0:3:1], [0:2048:1]} | slice | bytes 3145728 | tf_op jit(solution)/shard_map/slice | solution.py:45
  94.7 6.1 %multiply_subtract_fusion.1 = (f32[64,3,2048]{2,0,1:T(8,128)S(1)}, f32[64,3,2048]{2,0,1:T(8,128)S(1)}, f32[64,3,2048]{2,0,1:T(8,128)S(1)}, f32[64,3,2048]{2,0,1:T(8,128)S(1)}) fusion(f32[64,3,2048]{2,0,1:T(8,128)} %slice.425, f32[64,3,2048]{2,0,1:T(8,128)} %slice.431, f32[64,3,2048]{2,0,1:T(8,128)} %slice.423, f32[64,3,2048]{2,0,1:T(8,128)} %slice.430, ...), kind=kLoop, calls=%fused_computation.38 | loop fusion | flops 5505024 | bytes 18874368 | tf_op jit(solution)/shard_map/sub | solution.py:11
  103.7 4.4 %slice.432 = f32[31,3,2048]{2,0,1:T(8,128)} slice(f32[64,3,2048]{2,0,1:T(8,128)} %copy-done.12), slice={[2:64:2], [0:3:1], [0:2048:1]} | slice | bytes 1523712 | tf_op jit(solution)/shard_map/slice | solution.py:45
  108.2 4.4 %slice.511 = f32[31,3,2048]{2,0,1:T(8,128)} slice(f32[64,3,2048]{2,0,1:T(8,128)} %copy-done.11), slice={[2:64:2], [0:3:1], [0:2048:1]} | slice | bytes 1523712 | tf_op jit(solution)/shard_map/slice | solution.py:45
  112.6 4.4 %slice.440 = f32[32,3,2048]{2,0,1:T(8,128)} slice(f32[64,3,2048]{2,0,1:T(8,128)} %copy-done.12), slice={[0:63:2], [0:3:1], [0:2048:1]} | slice | bytes 1572864 | tf_op jit(solution)/shard_map/slice | solution.py:45
  117.0 4.3 %slice.433 = f32[32,3,2048]{2,0,1:T(8,128)} slice(f32[64,3,2048]{2,0,1:T(8,128)} %copy-done.12), slice={[1:64:2], [0:3:1], [0:2048:1]} | slice | bytes 1572864 | tf_op jit(solution)/shard_map/slice | solution.py:45
  121.3 4.4 %slice.441 = f32[32,3,2048]{2,0,1:T(8,128)} slice(f32[64,3,2048]{2,0,1:T(8,128)} %copy-done.11), slice={[0:63:2], [0:3:1], [0:2048:1]} | slice | bytes 1572864 | tf_op jit(solution)/shard_map/slice | solution.py:45
  125.7 4.4 %slice.435 = f32[32,3,2048]{2,0,1:T(8,128)} slice(f32[64,3,2048]{2,0,1:T(8,128)} %copy-done.11), slice={[1:64:2], [0:3:1], [0:2048:1]} | slice | bytes 1572864 | tf_op jit(solution)/shard_map/slice | solution.py:45
  245.7 6.2 %subtract_add_fusion = (f32[63,3,2048]{2,0,1:T(8,128)S(1)}, f32[63,3,2048]{2,0,1:T(8,128)S(1)}) fusion(f32[63,3,2048]{2,0,1:T(8,128)} %slice.521, f32[63,3,2048]{2,0,1:T(8,128)} %slice.517, f32[63,3,2048]{2,0,1:T(8,128)} %slice.422, f32[64,3,2048]{2,0,1:T(8,128)} %pad.193, f32[64,3,2048]{2,0,1:T(8,128)} %pad.192, f32[64,3,2048]{2,0,1:T(8,128)} %pad.195, ...), kind=kLoop, calls=%fused_computation.35 | loop fusion | flops 3870720 | bytes 15482880 | tf_op jit(solution)/shard_map/add | solution.py:13
  266.2 4.3 %pad.224 = f32[128,3,2048]{2,0,1:T(8,128)S(1)} pad(f32[64,3,2048]{2,0,1:T(8,128)} %pad_maximum_fusion.2, f32[]{:T(128)} %constant.7.clone.1), padding=0_1_1x0_0_0x0_0_0 | pad | bytes 4718596 | tf_op jit(solution)/shard_map/pad | solution.py:45
  270.5 7.6 %pad.196 = f32[128,3,2048]{2,0,1:T(8,128)} pad(f32[64,3,2048]{2,0,1:T(8,128)} %pad_maximum_fusion, f32[]{:T(128)} %constant.7.clone.1), padding=0_1_1x0_0_0x0_0_0 | pad | bytes 4718596 | tf_op jit(solution)/shard_map/pad | solution.py:45
  278.1 7.6 %pad.197 = f32[128,3,2048]{2,0,1:T(8,128)} pad(f32[64,3,2048]{2,0,1:T(8,128)} %add.427, f32[]{:T(128)} %constant.7.clone.1), padding=1_0_1x0_0_0x0_0_0 | pad | bytes 4718596 | tf_op jit(solution)/shard_map/pad | solution.py:45
  286.9 7.7 %pad.225 = f32[128,3,2048]{2,0,1:T(8,128)} pad(f32[64,3,2048]{2,0,1:T(8,128)} %add.430, f32[]{:T(128)} %constant.7.clone.1), padding=1_0_1x0_0_0x0_0_0 | pad | bytes 4718596 | tf_op jit(solution)/shard_map/pad | solution.py:45
  295.6 27.6 %all-gather = f32[32,3,2048]{2,1,0:T(4,128)} all-gather(f32[2,3,2048]{2,1,0:T(4,128)S(1)} %copy.12), channel_id=2, replica_groups=mesh['chan'=2,'seq'=16] {'seq'}, dimensions={0}, use_global_device_ids=true | all-gather | bytes 835584 | tf_op jit(solution)/shard_map/all_gather | solution.py:47
  323.2 47.0 %while.13 = (s32[]{:T(128)}, f32[3,2048]{1,0:T(4,128)S(1)}, f32[3,2048]{1,0:T(4,128)S(1)}, s32[16]{0:T(128)S(1)}, s32[]{:T(128)}, /*index=5*/f32[16,3]{1,0:T(8,1...) while((s32[]{:T(128)}, f32[3,2048]{1,0:T(4,128)S(1)}, ...), condition=%wide.region_2.3_spmd.clone, body=%wide.region_1.2_spmd.clone.sunk | while | flops 86021 | bytes 164057 | solution.py:64
  370.2 7.7 %pad.226 = f32[128,3,2048]{2,0,1:T(8,128)} pad(f32[64,3,2048]{2,0,1:T(8,128)} %pad_maximum_fusion.3, f32[]{:T(128)} %constant.7.clone.1), padding=0_1_1x0_0_0x0_0_0 | pad | bytes 4718596 | tf_op jit(solution)/shard_map/pad | solution.py:45
  377.9 7.8 %pad.222 = f32[128,3,2048]{2,0,1:T(8,128)} pad(f32[64,3,2048]{2,0,1:T(8,128)} %pad_maximum_fusion.1, f32[]{:T(128)} %constant.7.clone.1), padding=0_1_1x0_0_0x0_0_0 | pad | bytes 4718596 | tf_op jit(solution)/shard_map/pad | solution.py:45
  385.7 7.7 %pad.223 = f32[128,3,2048]{2,0,1:T(8,128)} pad(f32[64,3,2048]{2,0,1:T(8,128)} %add.448, f32[]{:T(128)} %constant.7.clone.1), padding=1_0_1x0_0_0x0_0_0 | pad | bytes 4718596 | tf_op jit(solution)/shard_map/pad | solution.py:45
  393.4 7.7 %pad.227 = f32[128,3,2048]{2,0,1:T(8,128)} pad(f32[64,3,2048]{2,0,1:T(8,128)} %add.450, f32[]{:T(128)} %constant.7.clone.1), padding=1_0_1x0_0_0x0_0_0 | pad | bytes 4718596 | tf_op jit(solution)/shard_map/pad | solution.py:45
  401.0 9.0 %fusion.7 = (bf16[128,1,3,2048]{3,0,2,1:T(8,128)(2,1)S(1)}, bf16[128,1,3,2048]{3,0,2,1:T(8,128)(2,1)S(1)}) fusion(f32[128,3,2048]{2,0,1:T(8,128)} %pad.196, f32[128,3,2048]{2,0,1:T(8,128)} %pad.197, f32[3,2048]{1,0:T(4,128)S(1)} %get-tuple-element.54, f32[3,2048]{1,0:T(4,128)S(1)} %get-tuple-element.53, f32[128,3,2048]{2,0,1:T(8,128)} %pad.226, ...), kind=kLoop, calls=%fused_computation.20 | loop fusion | flops 11010048 | bytes 28360704 | tf_op jit(solution)/shard_map/stack | solution.py:68
  410.3 4.9 %copy.14 = bf16[3,128,2,2048]{3,2,1,0:T(2,128)(2,1)} copy(bf16[3,128,2,2048]{3,1,0,2:T(8,128)(2,1)S(1)} %maximum_bitcast_fusion) | data formatting | bytes 6291456 | tf_op jit(solution)/shard_map/convert_element_type | solution.py:69
  (330 shorter events, 182.6 us)
Async XLA Ops:
  8.3 1.8 copy-start
  8.4 3.0 copy-start.1
  8.4 3.7 copy-start.2
  100.7 1.8 copy-start.12
  161.9 2.8 copy-start.21
  161.9 2.8 copy-start.22
  180.0 1.5 copy-start.39
  182.8 5.3 %copy-start.19 = (f32[15,3,2048]{2,0,1:T(8,128)S(1)}, f32[15,3,2048]{2,0,1:T(8,128)}, u32[]{:S(2)}) copy-start(f32[15,3,2048]{2,0,1:T(8,128)} %slice.442) | copy-start | bytes 1105924
  188.0 1.5 copy-start.20
  189.5 1.6 copy-start.35
  192.1 1.6 copy-start.34
  192.1 1.6 copy-start.33
  196.4 4.1 copy-start.23
  210.2 3.5 copy-start.17
  210.2 3.5 copy-start.18
  213.8 1.4 copy-start.15
  213.8 1.6 copy-start.16
  215.4 2.0 copy-start.13
  215.4 2.0 copy-start.14
  245.7 6.2 %copy-start.9 = (f32[64,3,2048]{2,0,1:T(8,128)S(1)}, f32[64,3,2048]{2,0,1:T(8,128)}, u32[]{:S(2)}) copy-start(f32[64,3,2048]{2,0,1:T(8,128)} %pad.194) | copy-start | bytes 4718596
  245.7 6.2 %copy-start.10 = (f32[64,3,2048]{2,0,1:T(8,128)S(1)}, f32[64,3,2048]{2,0,1:T(8,128)}, u32[]{:S(2)}) copy-start(f32[64,3,2048]{2,0,1:T(8,128)} %pad.195) | copy-start | bytes 4718596
  251.9 2.0 copy-start.7
  251.9 2.4 copy-start.8
  254.3 1.4 copy-start.31
  254.3 2.7 copy-start.5
  254.3 2.7 copy-start.6
  255.7 2.3 copy-start.3
  255.7 2.8 copy-start.4
  262.2 1.3 copy-start.29
  286.8 36.4 %copy-start.24 = (f32[3,2048]{1,0:T(4,128)S(1)}, f32[3,2048]{1,0:T(4,128)}, u32[]{:S(2)}) copy-start(f32[3,2048]{1,0:T(4,128)} %custom-call.1) | copy-start | bytes 73732
  286.8 36.4 %copy-start.25 = (f32[3,2048]{1,0:T(4,128)S(1)}, f32[3,2048]{1,0:T(4,128)}, u32[]{:S(2)}) copy-start(f32[3,2048]{1,0:T(4,128)} %custom-call) | copy-start | bytes 73732
  286.8 36.4 %copy-start.44 = (s32[16]{0:T(128)S(1)}, s32[16]{0:T(128)}, u32[]{:S(2)}) copy-start(s32[16]{0:T(128)} %iota.3) | copy-start | bytes 196
  (13 other events, 12.8 us)
where the time goes:
time: 421 us; the launch traced here: 415 us
  local copies, waits for them, and re-layouts  299 us (71%)
  other arithmetic  76.3 us (18%)
  blocking collectives  27.6 us (7%)
  loops' own time  11.4 us (3%)
    slice x91, local copies, waits for them, and re-layouts, shards(): lax.associative_scan(compose, items, axis=0)  155 us
    pad x48, local copies, waits for them, and re-layouts, shards(): lax.associative_scan(compose, items, axis=0)  106 us
    all_gather x1, blocking collectives, shards(): gathered = lax.all_gather(ends, 'seq', axis=0, tiled=True)  27.6 us
    add x26, other arithmetic, shards(): lax.associative_scan(compose, items, axis=0)  16.3 us
    select_n x16, other arithmetic, fold_block(): jnp.where(used, next_im, carry_im)  14.2 us
    another operation x1, loops' own time, shards(): lax.scan(fold_block, (zeros, zeros), (jnp.arange(blocks, dtype=jnp.int32)...  11.4 us
    mul x16, local copies, waits for them, and re-layouts, fold_block(): total_re = scale[:, None] * span_re[None, :]  11 us
    dynamic_slice x16, local copies, waits for them, and re-layouts, shards(): lax.scan(fold_block, (zeros, zeros), (jnp.arange(blocks, dtype=jnp.int32)...  10.4 us

commit v1 on v0

v1 whole, which is shorter than its diff:
```python
import functools

import jax
import jax.numpy as jnp
from jax import lax
from jax.experimental import pallas as pl
from jax.experimental.pallas import tpu as pltpu
from jax.sharding import PartitionSpec as P

LANES = 128


def coefficients(decay_rate, phase):
    magnitude = jnp.exp(-decay_rate)
    gamma = jnp.sqrt(-jnp.expm1(-2.0 * decay_rate))
    return (magnitude * jnp.cos(phase), magnitude * jnp.sin(phase), gamma)


def split_view(x):
    b, t, _, c = x.shape
    x = x.reshape(b, t, 2, c // LANES, LANES)
    return x.transpose(0, 1, 3, 2, 4).reshape(b, t, 2 * c // LANES, LANES)


def join_view(x):
    b, t, r, _ = x.shape
    x = x.reshape(b, t, r // 2, 2, LANES)
    return x.transpose(0, 1, 3, 2, 4).reshape(b, t, 2, r * LANES // 2)


def scan_chunk(keep, base, src, lre, lim, gam, state, store):
    batch, steps, rows2, _ = src.shape
    rows = rows2 // 2
    even = pl.ds(0, rows, stride=2)
    odd = pl.ds(1, rows, stride=2)
    for t in range(steps):
        for s in range(batch):
            hre, him = state[s]
            k = keep[s, base + t]
            hre, him = hre * k, him * k
            xre = src[s, t, even, :]
            xim = src[s, t, odd, :]
            if gam is not None:
                xre, xim = xre * gam, xim * gam
            nre = lre * hre - lim * him + xre
            nim = lre * him + lim * hre + xim
            state[s] = (nre, nim)
            if store:
                src[s, t, even, :] = nre
                src[s, t, odd, :] = nim
    return state


def end_kernel(length, keep, x, lre, lim, gam, end, flat, held):
    step = pl.program_id(0)
    batch, steps = x.shape[:2]

    @pl.when(step == 0)
    def _():
        held[...] = jnp.zeros_like(held)

    flat[...] = x[...].astype(jnp.float32)
    base = lax.axis_index("seq") * length + step * steps
    state = [(held[0, s], held[1, s]) for s in range(batch)]
    state = scan_chunk(keep, base, flat, lre[...], lim[...], None, state, False)
    for s in range(batch):
        held[0, s], held[1, s] = state[s]

    @pl.when(step == pl.num_programs(0) - 1)
    def _():
        for s in range(batch):
            end[0, s] = state[s][0] * gam[...]
            end[1, s] = state[s][1] * gam[...]


def full_kernel(length, keep, x, lre, lim, gam, start, out, flat, held):
    step = pl.program_id(0)
    batch, steps = x.shape[:2]

    @pl.when(step == 0)
    def _():
        held[...] = start[...]

    flat[...] = x[...].astype(jnp.float32)
    base = lax.axis_index("seq") * length + step * steps
    state = [(held[0, s], held[1, s]) for s in range(batch)]
    state = scan_chunk(keep, base, flat, lre[...], lim[...], gam[...], state, True)
    for s in range(batch):
        held[0, s], held[1, s] = state[s]
    out[...] = flat[...].astype(jnp.bfloat16)


def shards(inputs, decay_rate, phase, keep):
    lam_re, lam_im, gamma = coefficients(decay_rate, phase)
    batch, length, _, width = inputs.shape
    rows = width // LANES
    lre, lim, gam = (v.reshape(rows, LANES) for v in (lam_re, lam_im, gamma))
    x = split_view(inputs)
    steps = min(16, length)
    grid = (length // steps,)
    whole = pl.BlockSpec(memory_space=pltpu.VMEM)
    smem = pl.BlockSpec(memory_space=pltpu.SMEM)
    block = pl.BlockSpec((batch, steps, 2 * rows, LANES), lambda i: (0, i, 0, 0))
    scratch = [
        pltpu.VMEM((batch, steps, 2 * rows, LANES), jnp.float32),
        pltpu.VMEM((2, batch, rows, LANES), jnp.float32),
    ]
    ends = pl.pallas_call(
        functools.partial(end_kernel, length),
        grid=grid,
        out_shape=jax.ShapeDtypeStruct((2, batch, rows, LANES), jnp.float32),
        in_specs=[smem, block, whole, whole, whole],
        out_specs=whole,
        scratch_shapes=scratch,
        name="ends",
    )(keep, x, lre, lim, gam)

    me = lax.axis_index("seq")
    blocks = lax.axis_size("seq")
    gathered = lax.all_gather(ends[None], "seq", axis=0, tiled=True)
    block_keep = jnp.prod(keep.reshape(batch, blocks, length), axis=2)
    span_mag = jnp.exp(-(length * 1.0) * decay_rate)
    span_re = (span_mag * jnp.cos(length * 1.0 * phase)).reshape(rows, LANES)
    span_im = (span_mag * jnp.sin(length * 1.0 * phase)).reshape(rows, LANES)
    carry_re = jnp.zeros((batch, rows, LANES), jnp.float32)
    carry_im = carry_re
    for b in range(blocks):
        scale = block_keep[:, b][:, None, None]
        tre, tim = scale * span_re, scale * span_im
        nre = tre * carry_re - tim * carry_im + gathered[b, 0]
        nim = tre * carry_im + tim * carry_re + gathered[b, 1]
        carry_re = jnp.where(b < me, nre, carry_re)
        carry_im = jnp.where(b < me, nim, carry_im)
    carry = jnp.stack([carry_re, carry_im])

    out = pl.pallas_call(
        functools.partial(full_kernel, length),
        grid=grid,
        out_shape=jax.ShapeDtypeStruct((batch, length, 2 * rows, LANES), jnp.bfloat16),
        in_specs=[smem, block, whole, whole, whole, whole],
        out_specs=block,
        scratch_shapes=scratch,
        name="full",
    )(keep, x, lre, lim, gam, carry)
    return join_view(out)


def solution(mesh):
    in_specs = (P(None, "seq", None, "chan"), P("chan"), P("chan"), P())
    out_specs = P(None, "seq", None, "chan")
    return jax.shard_map(shards, mesh=mesh, in_specs=in_specs, out_specs=out_specs, check_vma=False)
```

time: 421 us -> 43.4 us (0.10); the launches traced: 415 us -> 42.9 us
  local copies, waits for them, and re-layouts: 299 us -> 0.44 us
  other arithmetic: 76.3 us -> 3.39 us
  Pallas kernels: 0 us -> 13.3 us
  loops' own time: 11.4 us -> 0 us
    slice x91 -> x1, local copies, waits for them, and re-layouts: 155 us -> 0.44 us  [shards(): scale = block_keep[:, b][:, None, None]]
    pad x48 -> x0, local copies, waits for them, and re-layouts: 106 us -> none  [shards(): lax.associative_scan(compose, items, axis=0)]
    add x41 -> x0, other arithmetic: 32.5 us -> none  [the longest x26 16.3 us: shards(): lax.associative_scan(compose, items, axis=0)]
    select_n x16 -> x4, other arithmetic: 14.2 us -> 0.48 us  [the longest x3 0.39 us: shards(): carry_re = jnp.where(b < me, nre, carry_re)]
    pallas_call x0 -> x2, Pallas kernels: none -> 13.3 us  [the longest x1 7.24 us: shards(): pl.pallas_call(functools.partial(full_kernel, length), grid=grid, out_sha...]
    another operation x1 -> x0, loops' own time: 11.4 us -> none  [shards(): lax.scan(fold_block, (zeros, zeros), (jnp.arange(blocks, dtype=jnp.int32)...]
    mul x16 -> x0, local copies, waits for them, and re-layouts: 11 us -> none  [fold_block(): total_re = scale[:, None] * span_re[None, :]]
    dynamic_slice x16 -> x0, local copies, waits for them, and re-layouts: 10.4 us -> none  [shards(): lax.scan(fold_block, (zeros, zeros), (jnp.arange(blocks, dtype=jnp.int32)...]
where the time goes in v1:
time: 43.4 us; the launch traced here: 42.9 us
  blocking collectives  25.7 us (59%)
  Pallas kernels  13.3 us (31%)
  other arithmetic  3.39 us (8%)
  local copies, waits for them, and re-layouts  0.44 us (1%)
    all_gather x1, blocking collectives, shards(): gathered = lax.all_gather(ends[None], 'seq', axis=0, tiled=True)  25.7 us
    pallas_call x1, Pallas kernels, shards(): pl.pallas_call(functools.partial(full_kernel, length), grid=grid, out_sha...  7.24 us
    pallas_call x1, Pallas kernels, shards(): pl.pallas_call(functools.partial(end_kernel, length), grid=grid, out_shap...  6.08 us
    mul x1, other arithmetic, shards(): tre, tim = (scale * span_re, scale * span_im)  1.39 us
    reduce_prod x1, other arithmetic, shards(): block_keep = jnp.prod(keep.reshape(batch, blocks, length), axis=2)  0.89 us

profile of v1, /device:TPU:0, one launch (start us, length us, event | category | flops | bytes accessed | tf_op | source)
XLA Modules:
  0.0 42.9 jit_solution(16640155911448365183)
XLA Ops:
  0.0 0.9 %bitcast_reduce_fusion = f32[3,16]{1,0:T(4,128)S(1)} fusion(f32[1,3,16,128]{3,1,2,0:T(4,128)} %bitcast.282), kind=kLoop, calls=%fused_computation.151 | loop fusion | flops 6096 | bytes 24768 | tf_op jit(solution)/shard_map/reduce_prod | solution.py:121
  0.9 0.4 %slice_reduce_fusion.14 = (f32[3]{0:T(128)S(1)}, f32[3]{0:T(128)S(1)}, f32[3]{0:T(128)S(1)}, f32[3]{0:T(128)S(1)}, f32[3]{0:T(128)S(1)}, /*index=5*/f32[3]{0:T(1...) fusion(f32[3,16]{1,0:T(4,128)S(1)} %bitcast_reduce_fusion), kind=kLoop, calls=%fused_computation.211 | loop fusion | bytes 384 | tf_op jit(solution)/shard_map/slice | solution.py:128
  1.3 1.4 %multiply_bitcast_fusion.1 = (f32[16,128]{1,0:T(8,128)S(1)}, f32[16,128]{1,0:T(8,128)S(1)}, f32[16,128]{1,0:T(8,128)}, f32[16,128]{1,0:T(8,128)}, f32[16,128]{1,0:T(8,128)}) fusion(f32[2048]{0:T(1024)} %param.6, f32[2048]{0:T(1024)} %param.5), kind=kLoop, calls=%fused_computation.191 | loop fusion | flops 18432 | bytes 57344 | tf_op jit(solution)/shard_map/mul | solution.py:129
  2.7 6.1 %ends.1 = f32[2,3,16,128]{3,2,1,0:T(8,128)} custom-call(f32[3,2048]{1,0:T(4,128)} %keep.3, bf16[3,128,32,128]{3,2,1,0:T(8,128)(2,1)} %bitcast.276, f32[16,128]{1,0:T(8,128)} %get-tuple-element.32.lre, f32[16,128]{1,0:T(8,128)} %get-tuple-element.33.lim, f32[16,128]{1,0:T(8,128)} %get-tuple-element.34.gam), custom_call_target="tpu_custom_call" | custom-call | tf_op jit(solution)/shard_map/ends/pallas_call | solution.py:108
  8.8 25.7 %all-gather = f32[32,3,16,128]{3,2,1,0:T(8,128)S(1)} all-gather(f32[2,3,16,128]{3,2,1,0:T(8,128)} %ends.1), channel_id=2, replica_groups=mesh['chan'=2,'seq'=16] {'seq'}, dimensions={0}, use_global_device_ids=true | all-gather | bytes 835584 | tf_op jit(solution)/shard_map/all_gather | solution.py:120
  34.5 0.1 fusion.50
  34.7 0.1 fusion.26
  34.8 0.1 fusion.2
  34.9 0.1 fusion.5
  35.0 0.6 %pad_maximum_fusion.start = f32[2,3,16,128]{3,2,1,0:T(8,128)} fusion(f32[1,3,16,128]{3,2,1,0:T(8,128)S(1)} %fusion.5, f32[1,3,16,128]{3,2,1,0:T(8,128)S(1)} %get-tuple-element.21), kind=kLoop, calls=%fused_computation | loop fusion | flops 12288 | bytes 98304 | tf_op jit(solution)/shard_map/stack | solution.py:134
  35.7 7.2 %full.1 = bf16[3,128,32,128]{3,2,1,0:T(8,128)(2,1)} custom-call(f32[3,2048]{1,0:T(4,128)} %keep.3, bf16[3,128,32,128]{3,2,1,0:T(8,128)(2,1)} %bitcast.277, f32[16,128]{1,0:T(8,128)} %get-tuple-element.32.lre, f32[16,128]{1,0:T(8,128)} %get-tuple-element.33.lim, f32[16,128]{1,0:T(8,128)} %get-tuple-element.34.gam, f32[2,3,16,128]{3,2,1,0:T(8,128)} %pad_maximum_fusion.start), custom_call_target="tpu_custom_call" | custom-call | tf_op jit(solution)/shard_map/full/pallas_call | solution.py:136

commit v2 on v1

--- a/solution.py
+++ b/solution.py
@@ -51,16 +51,135 @@
     return state
 
 
-def end_kernel(length, keep, x, lre, lim, gam, end, flat, held):
+def cmul(a, b):
+    return a[0] * b[0] - a[1] * b[1], a[0] * b[1] + a[1] * b[0]
+
+
+def exchange(group, blocks, block_keep, span, own, near, total, far, spread, back, sems, carry):
+    send_a, recv_a, send_b, recv_b, send_c, recv_c = sems
+    batch = own.shape[2]
+    me = lax.axis_index("seq")
+    part = lax.rem(me, group)
+    at = me // group
+    groups = blocks // group
+
+    def member(d):
+        return lax.rem(part + d, group)
+
+    def copy(src, dst, send, recv, target):
+        return pltpu.make_async_remote_copy(
+            src_ref=src, dst_ref=dst, send_sem=send, recv_sem=recv,
+            device_id={"seq": target}, device_id_type=pl.DeviceIdType.MESH,
+        )
+
+    def copy_a(d):
+        return copy(own.at[member(d)], near.at[d], send_a.at[d], recv_a.at[d], at * group + member(d))
+
+    def copy_b(d):
+        return copy(total, far.at[d], send_b.at[d], recv_b.at[d], me + d * group)
+
+    def copy_c(d):
+        return copy(spread.at[d], back.at[d], send_c.at[d], recv_c.at[d], at * group + member(d))
+
+    for d in range(group - 1, 0, -1):
+        copy_a(d).start()
+    near[0] = own[part]
+    lam = (span[part, 0], span[part, 1])
+    powers = [None, lam]
+    for _ in range(group - 1):
+        powers.append(cmul(powers[-1], lam))
+    for d in range(1, group):
+        copy_a(d).wait_recv()
+
+    inner = [[None] * batch for _ in range(group + 1)]
+    scales = [[None] * batch for _ in range(group + 1)]
+    for i in range(group):
+        slot = lax.rem(part + group - i, group)
+        for s in range(batch):
+            k = block_keep[s, at * group + i]
+            end = (near[slot, 0, s], near[slot, 1, s])
+            if i == 0:
+                inner[1][s], scales[1][s] = end, k
+            else:
+                step = cmul((k * lam[0], k * lam[1]), inner[i][s])
+                inner[i + 1][s] = (step[0] + end[0], step[1] + end[1])
+                scales[i + 1][s] = scales[i][s] * k
+    for s in range(batch):
+        total[0, s], total[1, s] = inner[group][s]
+    for d in range(groups - 1, 0, -1):
+
+        @pl.when(at + d < groups)
+        def _(d=d):
+            copy_b(d).start()
+
+    for m in range(group):
+        slot = lax.rem(m + group - part, group)
+        for s in range(batch):
+            if m == 0:
+                zero = jnp.zeros_like(lam[0])
+                spread[slot, 0, s], spread[slot, 1, s] = zero, zero
+            else:
+                spread[slot, 0, s], spread[slot, 1, s] = inner[m][s]
+    far[0] = jnp.zeros(far.shape[1:], jnp.float32)
+    for d in range(groups - 1, 0, -1):
+
+        @pl.when(at - d >= 0)
+        def _(d=d):
+            copy_b(d).wait_recv()
+            for s in range(batch):
+                k = jnp.float32(1)
+                for i in range(group):
+                    k = k * block_keep[s, (at - d) * group + i]
+                step = cmul((k * powers[group][0], k * powers[group][1]), (far[0, 0, s], far[0, 1, s]))
+                far[0, 0, s] = step[0] + far[d, 0, s]
+                far[0, 1, s] = step[1] + far[d, 1, s]
+
+    entry = [(far[0, 0, s], far[0, 1, s]) for s in range(batch)]
+    for m in range(group):
+        slot = lax.rem(m + group - part, group)
+        for s in range(batch):
+            if m == 0:
+                step = entry[s]
+            else:
+                step = cmul((scales[m][s] * powers[m][0], scales[m][s] * powers[m][1]), entry[s])
+            spread[slot, 0, s] += step[0]
+            spread[slot, 1, s] += step[1]
+    for d in range(group - 1, 0, -1):
+        copy_c(d).start()
+    carry[part] = spread[0]
+    for d in range(1, group):
+        copy_c(d).wait_recv()
+        carry[lax.rem(part + group - d, group)] = back[d]
+    for d in range(1, group):
+        copy_a(d).wait_send()
+        copy_c(d).wait_send()
+    for d in range(1, groups):
+
+        @pl.when(at + d < groups)
+        def _(d=d):
+            copy_b(d).wait_send()
+
+
+def end_kernel(length, group, blocks, keep, block_keep, x, lre, lim, gam, span, carry, flat, held, own, near, total, far, spread, back, *sems):
     step = pl.program_id(0)
     batch, steps = x.shape[:2]
+    me = lax.axis_index("seq")
+    barrier = pltpu.get_barrier_semaphore()
+    peers = group - 1 + blocks // group - 1
 
     @pl.when(step == 0)
     def _():
         held[...] = jnp.zeros_like(held)
+        first = me // group * group
+        for d in range(1, group):
+            peer = first + lax.rem(me + d, group)
+            pl.semaphore_signal(barrier, inc=1, device_id={"seq": peer}, device_id_type=pl.DeviceIdType.MESH)
+        for d in range(1, blocks // group):
+            peer = lax.rem(me + d * group, blocks)
+            pl.semaphore_signal(barrier, inc=1, device_id={"seq": peer}, device_id_type=pl.DeviceIdType.MESH)
 
     flat[...] = x[...].astype(jnp.float32)
-    base = lax.axis_index("seq") * length + step * steps
+    base = me * length + step * steps
     state = [(held[0, s], held[1, s]) for s in range(batch)]
     state = scan_chunk(keep, base, flat, lre[...], lim[...], None, state, False)
     for s in range(batch):
@@ -68,9 +187,14 @@
 
     @pl.when(step == pl.num_programs(0) - 1)
     def _():
-        for s in range(batch):
-            end[0, s] = state[s][0] * gam[...]
-            end[1, s] = state[s][1] * gam[...]
+        part_rows = own.shape[3]
+        for s in range(batch):
+            for c in range(2):
+                value = state[s][c] * gam[...]
+                for p in range(group):
+                    own[p, c, s] = value[p * part_rows : (p + 1) * part_rows]
+        pl.semaphore_wait(barrier, peers)
+        exchange(group, blocks, block_keep, span, own, near, total, far, spread, back, sems, carry)
 
 
 def full_kernel(length, keep, x, lre, lim, gam, start, out, flat, held):
@@ -79,7 +203,9 @@
 
     @pl.when(step == 0)
     def _():
-        held[...] = start[...]
+        group, _, _, part_rows, _ = start.shape
+        for p in range(group):
+            held[:, :, p * part_rows : (p + 1) * part_rows] = start[p]
 
     flat[...] = x[...].astype(jnp.float32)
     base = lax.axis_index("seq") * length + step * steps
@@ -105,33 +231,35 @@
         pltpu.VMEM((batch, steps, 2 * rows, LANES), jnp.float32),
         pltpu.VMEM((2, batch, rows, LANES), jnp.float32),
     ]
-    ends = pl.pallas_call(
-        functools.partial(end_kernel, length),
-        grid=grid,
-        out_shape=jax.ShapeDtypeStruct((2, batch, rows, LANES), jnp.float32),
-        in_specs=[smem, block, whole, whole, whole],
-        out_specs=whole,
-        scratch_shapes=scratch,
-        name="ends",
-    )(keep, x, lre, lim, gam)
-
-    me = lax.axis_index("seq")
     blocks = lax.axis_size("seq")
-    gathered = lax.all_gather(ends[None], "seq", axis=0, tiled=True)
+    group = 4
+    groups = blocks // group
     block_keep = jnp.prod(keep.reshape(batch, blocks, length), axis=2)
     span_mag = jnp.exp(-(length * 1.0) * decay_rate)
-    span_re = (span_mag * jnp.cos(length * 1.0 * phase)).reshape(rows, LANES)
-    span_im = (span_mag * jnp.sin(length * 1.0 * phase)).reshape(rows, LANES)
-    carry_re = jnp.zeros((batch, rows, LANES), jnp.float32)
-    carry_im = carry_re
-    for b in range(blocks):
-        scale = block_keep[:, b][:, None, None]
-        tre, tim = scale * span_re, scale * span_im
-        nre = tre * carry_re - tim * carry_im + gathered[b, 0]
-        nim = tre * carry_im + tim * carry_re + gathered[b, 1]
-        carry_re = jnp.where(b < me, nre, carry_re)
-        carry_im = jnp.where(b < me, nim, carry_im)
-    carry = jnp.stack([carry_re, carry_im])
+    span_re = (span_mag * jnp.cos(length * 1.0 * phase)).reshape(group, rows // group, LANES)
+    span_im = (span_mag * jnp.sin(length * 1.0 * phase)).reshape(group, rows // group, LANES)
+    span = jnp.stack([span_re, span_im], axis=1)
+    piece = (2, batch, rows // group, LANES)
+    dma = pltpu.SemaphoreType.DMA
+    carry = pl.pallas_call(
+        functools.partial(end_kernel, length, group, blocks),
+        grid=grid,
+        out_shape=jax.ShapeDtypeStruct((group,) + piece, jnp.float32),
+        in_specs=[smem, smem, block, whole, whole, whole, whole],
+        out_specs=whole,
+        scratch_shapes=scratch
+        + [
+            pltpu.VMEM((group,) + piece, jnp.float32),
+            pltpu.VMEM((group,) + piece, jnp.float32),
+            pltpu.VMEM(piece, jnp.float32),
+            pltpu.VMEM((groups,) + piece, jnp.float32),
+            pltpu.VMEM((group,) + piece, jnp.float32),
+            pltpu.VMEM((group,) + piece, jnp.float32),
+            dma((group,)), dma((group,)), dma((groups,)), dma((groups,)), dma((group,)), dma((group,)),
+        ],
+        compiler_params=pltpu.CompilerParams(collective_id=0, has_side_effects=True),
+        name="ends",
+    )(keep, block_keep, x, lre, lim, gam, span)
 
     out = pl.pallas_call(
         functools.partial(full_kernel, length),

time: 43.4 us -> 25.9 us (0.60)
  the two profiles are of different devices: /device:TPU:0 before, /device:TPU:18 now
where the time goes in v2:
time: 25.9 us; the launch traced here: 25.4 us
  Pallas kernels  21.9 us (85%)
  other arithmetic  3.49 us (13%)
    pallas_call x1, Pallas kernels, shards(): pl.pallas_call(functools.partial(end_kernel, length, group, blocks), grid...  14.6 us
    pallas_call x1, Pallas kernels, shards(): pl.pallas_call(functools.partial(full_kernel, length), grid=grid, out_sha...  7.29 us
    reduce_prod x1, other arithmetic, shards(): block_keep = jnp.prod(keep.reshape(batch, blocks, length), axis=2)  1.5 us
    mul x1, other arithmetic, shards(): span_mag * jnp.cos(length * 1.0 * phase)  1.38 us
    another operation x1, other arithmetic, shards(): span = jnp.stack([span_re, span_im], axis=1)  0.61 us

profile of v2, /device:TPU:18, one launch (start us, length us, event | category | flops | bytes accessed | tf_op | source)
XLA Modules:
  0.0 25.4 jit_solution(1000601972325771632)
XLA Ops:
  0.0 1.5 %bitcast_reduce_fusion.block_keep = f32[3,16]{1,0:T(4,128)} fusion(f32[1,3,16,128]{3,1,2,0:T(4,128)} %bitcast.23), kind=kLoop, calls=%fused_computation | loop fusion | flops 6096 | bytes 24768 | tf_op jit(solution)/shard_map/reduce_prod | solution.py:237
  1.5 1.4 %cosine_multiply_fusion = (f32[2048]{0:T(1024)S(1)}, f32[2048]{0:T(1024)S(1)}, f32[16,128]{1,0:T(8,128)}, f32[16,128]{1,0:T(8,128)}, f32[16,128]{1,0:T(8,128)}) fusion(f32[2048]{0:T(1024)} %param.6, f32[2048]{0:T(1024)} %param.5), kind=kLoop, calls=%fused_computation.3 | loop fusion | flops 18432 | bytes 57344 | tf_op jit(solution)/shard_map/mul | solution.py:239
  2.9 0.6 %pad_maximum_fusion.span = f32[4,2,4,128]{3,2,1,0:T(4,128)} fusion(f32[4,1,4,128]{3,2,1,0:T(4,128)S(1)} %bitcast.25, f32[4,1,4,128]{3,2,1,0:T(4,128)S(1)} %bitcast.24), kind=kLoop, calls=%fused_computation.1 | loop fusion | flops 4096 | bytes 32768 | tf_op jit(solution)/shard_map/stack | solution.py:241
  3.5 14.6 %ends.1.start = f32[4,2,3,4,128]{4,3,2,1,0:T(4,128)} custom-call(f32[3,2048]{1,0:T(4,128)} %keep.3, f32[3,16]{1,0:T(4,128)} %bitcast_reduce_fusion.block_keep, bf16[3,128,32,128]{3,2,1,0:T(8,128)(2,1)} %bitcast.21, f32[16,128]{1,0:T(8,128)} %get-tuple-element.7.lre, f32[16,128]{1,0:T(8,128)} %get-tuple-element.8.lim, f32[16,128]{1,0:T(8,128)} %get-tuple-element.9.gam, ...), custom_call_target="tpu_custom_call" | custom-call | tf_op jit(solution)/shard_map/ends/pallas_call | solution.py:244
  18.1 7.3 %full.1 = bf16[3,128,32,128]{3,2,1,0:T(8,128)(2,1)} custom-call(f32[3,2048]{1,0:T(4,128)} %keep.3, bf16[3,128,32,128]{3,2,1,0:T(8,128)(2,1)} %bitcast.22, f32[16,128]{1,0:T(8,128)} %get-tuple-element.7.lre, f32[16,128]{1,0:T(8,128)} %get-tuple-element.8.lim, f32[16,128]{1,0:T(8,128)} %get-tuple-element.9.gam, f32[4,2,3,4,128]{4,3,2,1,0:T(4,128)} %ends.1.start), custom_call_target="tpu_custom_call" | custom-call | tf_op jit(solution)/shard_map/full/pallas_call | solution.py:264

commit v3 on v2

--- a/solution.py
+++ b/solution.py
@@ -8,11 +8,16 @@
 from jax.sharding import PartitionSpec as P
 
 LANES = 128
+GRANT = 12 * 1024 * 1024
 
 
 def coefficients(decay_rate, phase):
     magnitude = jnp.exp(-decay_rate)
-    gamma = jnp.sqrt(-jnp.expm1(-2.0 * decay_rate))
+    y = 2.0 * decay_rate
+    series = 1.0 - y / 6.0 * (1.0 - y / 7.0)
+    for n in (5.0, 4.0, 3.0, 2.0):
+        series = 1.0 - y / n * series
+    gamma = jnp.sqrt(jnp.where(y < 0.0625, y * series, 1.0 - jnp.exp(-y)))
     return (magnitude * jnp.cos(phase), magnitude * jnp.sin(phase), gamma)
 
 
@@ -55,7 +60,7 @@
     return a[0] * b[0] - a[1] * b[1], a[0] * b[1] + a[1] * b[0]
 
 
-def exchange(group, blocks, block_keep, span, own, near, total, far, spread, back, sems, carry):
+def exchange(length, group, blocks, keep_rows, coef, prods, span, own, near, total, far, spread, back, sems, carry):
     send_a, recv_a, send_b, recv_b, send_c, recv_c = sems
     batch = own.shape[2]
     me = lax.axis_index("seq")
@@ -84,6 +89,21 @@
     for d in range(group - 1, 0, -1):
         copy_a(d).start()
     near[0] = own[part]
+    power = (coef[0], coef[1])
+    done, left = None, length
+    while left:
+        if left % 2:
+            done = power if done is None else cmul(done, power)
+        left //= 2
+        if left:
+            power = cmul(power, power)
+    part_rows = own.shape[3]
+    for p in range(group):
+        for c in range(2):
+            span[p, c] = done[c][p * part_rows : (p + 1) * part_rows]
+    for b in range(blocks):
+        logs = jnp.log(keep_rows[:, b * length : (b + 1) * length])
+        prods[b] = jnp.broadcast_to(jnp.exp(jnp.sum(logs, axis=1, keepdims=True)), prods.shape[1:])
     lam = (span[part, 0], span[part, 1])
     powers = [None, lam]
     for _ in range(group - 1):
@@ -96,7 +116,7 @@
     for i in range(group):
         slot = lax.rem(part + group - i, group)
         for s in range(batch):
-            k = block_keep[s, at * group + i]
+            k = prods[at * group + i, pl.ds(s, 1), :]
             end = (near[slot, 0, s], near[slot, 1, s])
             if i == 0:
                 inner[1][s], scales[1][s] = end, k
@@ -127,9 +147,9 @@
         def _(d=d):
             copy_b(d).wait_recv()
             for s in range(batch):
-                k = jnp.float32(1)
-                for i in range(group):
-                    k = k * block_keep[s, (at - d) * group + i]
+                k = prods[(at - d) * group, pl.ds(s, 1), :]
+                for i in range(1, group):
+                    k = k * prods[(at - d) * group + i, pl.ds(s, 1), :]
                 step = cmul((k * powers[group][0], k * powers[group][1]), (far[0, 0, s], far[0, 1, s]))
                 far[0, 0, s] = step[0] + far[d, 0, s]
                 far[0, 1, s] = step[1] + far[d, 1, s]
@@ -160,7 +180,7 @@
             copy_b(d).wait_send()
 
 
-def end_kernel(length, group, blocks, keep, block_keep, x, lre, lim, gam, span, carry, flat, held, own, near, total, far, spread, back, *sems):
+def end_kernel(length, group, blocks, keep, keep_rows, x, decay, phase, carry, coef, flat, held, prods, span, own, near, total, far, spread, back, *sems):
     step = pl.program_id(0)
     batch, steps = x.shape[:2]
     me = lax.axis_index("seq")
@@ -170,6 +190,7 @@
     @pl.when(step == 0)
     def _():
         held[...] = jnp.zeros_like(held)
+        coef[0], coef[1], coef[2] = coefficients(decay[...], phase[...])
         first = me // group * group
         for d in range(1, group):
             peer = first + lax.rem(me + d, group)
@@ -181,7 +202,7 @@
     flat[...] = x[...].astype(jnp.float32)
     base = me * length + step * steps
     state = [(held[0, s], held[1, s]) for s in range(batch)]
-    state = scan_chunk(keep, base, flat, lre[...], lim[...], None, state, False)
+    state = scan_chunk(keep, base, flat, coef[0], coef[1], None, state, False)
     for s in range(batch):
         held[0, s], held[1, s] = state[s]
 
@@ -190,14 +211,14 @@
         part_rows = own.shape[3]
         for s in range(batch):
             for c in range(2):
-                value = state[s][c] * gam[...]
+                value = state[s][c] * coef[2]
                 for p in range(group):
                     own[p, c, s] = value[p * part_rows : (p + 1) * part_rows]
         pl.semaphore_wait(barrier, peers)
-        exchange(group, blocks, block_keep, span, own, near, total, far, spread, back, sems, carry)
-
-
-def full_kernel(length, keep, x, lre, lim, gam, start, out, flat, held):
+        exchange(length, group, blocks, keep_rows, coef, prods, span, own, near, total, far, spread, back, sems, carry)
+
+
+def full_kernel(length, keep, x, coef, start, out, flat, held):
     step = pl.program_id(0)
     batch, steps = x.shape[:2]
 
@@ -210,17 +231,15 @@
     flat[...] = x[...].astype(jnp.float32)
     base = lax.axis_index("seq") * length + step * steps
     state = [(held[0, s], held[1, s]) for s in range(batch)]
-    state = scan_chunk(keep, base, flat, lre[...], lim[...], gam[...], state, True)
+    state = scan_chunk(keep, base, flat, coef[0], coef[1], coef[2], state, True)
     for s in range(batch):
         held[0, s], held[1, s] = state[s]
     out[...] = flat[...].astype(jnp.bfloat16)
 
 
 def shards(inputs, decay_rate, phase, keep):
-    lam_re, lam_im, gamma = coefficients(decay_rate, phase)
     batch, length, _, width = inputs.shape
     rows = width // LANES
-    lre, lim, gam = (v.reshape(rows, LANES) for v in (lam_re, lam_im, gamma))
     x = split_view(inputs)
     steps = min(16, length)
     grid = (length // steps,)
@@ -234,21 +253,21 @@
     blocks = lax.axis_size("seq")
     group = 4
     groups = blocks // group
-    block_keep = jnp.prod(keep.reshape(batch, blocks, length), axis=2)
-    span_mag = jnp.exp(-(length * 1.0) * decay_rate)
-    span_re = (span_mag * jnp.cos(length * 1.0 * phase)).reshape(group, rows // group, LANES)
-    span_im = (span_mag * jnp.sin(length * 1.0 * phase)).reshape(group, rows // group, LANES)
-    span = jnp.stack([span_re, span_im], axis=1)
     piece = (2, batch, rows // group, LANES)
     dma = pltpu.SemaphoreType.DMA
-    carry = pl.pallas_call(
+    carry, coef = pl.pallas_call(
         functools.partial(end_kernel, length, group, blocks),
         grid=grid,
-        out_shape=jax.ShapeDtypeStruct((group,) + piece, jnp.float32),
-        in_specs=[smem, smem, block, whole, whole, whole, whole],
-        out_specs=whole,
+        out_shape=(
+            jax.ShapeDtypeStruct((group,) + piece, jnp.float32),
+            jax.ShapeDtypeStruct((3, rows, LANES), jnp.float32),
+        ),
+        in_specs=[smem, whole, block, whole, whole],
+        out_specs=(whole, whole),
         scratch_shapes=scratch
         + [
+            pltpu.VMEM((blocks, batch, LANES), jnp.float32),
+            pltpu.VMEM((group, 2, rows // group, LANES), jnp.float32),
             pltpu.VMEM((group,) + piece, jnp.float32),
             pltpu.VMEM((group,) + piece, jnp.float32),
             pltpu.VMEM(piece, jnp.float32),
@@ -257,19 +276,20 @@
             pltpu.VMEM((group,) + piece, jnp.float32),
             dma((group,)), dma((group,)), dma((groups,)), dma((groups,)), dma((group,)), dma((group,)),
         ],
-        compiler_params=pltpu.CompilerParams(collective_id=0, has_side_effects=True),
+        compiler_params=pltpu.CompilerParams(collective_id=0, has_side_effects=True, vmem_limit_bytes=GRANT),
         name="ends",
-    )(keep, block_keep, x, lre, lim, gam, span)
+    )(keep, keep, x, decay_rate.reshape(rows, LANES), phase.reshape(rows, LANES))
 
     out = pl.pallas_call(
         functools.partial(full_kernel, length),
         grid=grid,
         out_shape=jax.ShapeDtypeStruct((batch, length, 2 * rows, LANES), jnp.bfloat16),
-        in_specs=[smem, block, whole, whole, whole, whole],
+        in_specs=[smem, block, whole, whole],
         out_specs=block,
         scratch_shapes=scratch,
+        compiler_params=pltpu.CompilerParams(vmem_limit_bytes=GRANT),
         name="full",
-    )(keep, x, lre, lim, gam, carry)
+    )(keep, x, coef, carry)
     return join_view(out)
 
 

time: 25.9 us -> 23 us (0.89)
  the two profiles are of different devices: /device:TPU:18 before, /device:TPU:12 now
where the time goes in v3:
time: 23 us; the launch traced here: 22.7 us
  Pallas kernels  18.6 us (81%)
  local copies, waits for them, and re-layouts  4.04 us (18%)
    pallas_call x1, Pallas kernels, shards(): pl.pallas_call(functools.partial(end_kernel, length, group, blocks), grid...  13.1 us
    pallas_call x1, Pallas kernels, shards(): pl.pallas_call(functools.partial(full_kernel, length), grid=grid, out_sha...  5.51 us
    unnamed x8, local copies, waits for them, and re-layouts  4.04 us

profile of v3, /device:TPU:12, one launch (start us, length us, event | category | flops | bytes accessed | tf_op | source)
XLA Modules:
  0.0 22.7 jit_solution(17157218564497429203)
XLA Ops:
  0.0 0.0 copy-start
  0.0 1.9 %copy-done = bf16[3,128,2,2048]{3,2,1,0:T(2,128)(2,1)S(1)} copy-done((bf16[3,128,2,2048]{3,2,1,0:T(2,128)(2,1)S(1)}, bf16[3,128,2,2048]{3,2,1,0:T(2,128)(2,1)}, u32[]{:S(2)}) %copy-start) | copy-done | bytes 3145752
  1.9 0.0 copy-start.1
  1.9 0.8 %copy-done.1 = f32[3,2048]{1,0:T(4,128)S(1)} copy-done((f32[3,2048]{1,0:T(4,128)S(1)}, f32[3,2048]{1,0:T(4,128)}, u32[]{:S(2)}) %copy-start.1) | copy-done | bytes 24600
  2.6 0.0 copy-start.2
  2.7 0.7 %copy-done.2 = f32[2048]{0:T(1024)S(1)} copy-done((f32[2048]{0:T(1024)S(1)}, f32[2048]{0:T(1024)}, u32[]{:S(2)}) %copy-start.2) | copy-done | bytes 8216
  3.3 0.0 copy-start.3
  3.3 0.7 %copy-done.3 = f32[2048]{0:T(1024)S(1)} copy-done((f32[2048]{0:T(1024)S(1)}, f32[2048]{0:T(1024)}, u32[]{:S(2)}) %copy-start.3) | copy-done | bytes 8216
  4.0 13.1 %ends.1 = (f32[4,2,3,4,128]{4,3,2,1,0:T(4,128)S(1)}, f32[3,16,128]{2,1,0:T(8,128)S(1)}) custom-call(f32[3,2048]{1,0:T(4,128)S(1)} %copy-done.1, f32[3,2048]{1,0:T(4,128)S(1)} %copy-done.1, bf16[3,128,32,128]{3,2,1,0:T(8,128)(2,1)S(1)} %bitcast.12, f32[16,128]{1,0:T(8,128)S(1)} %bitcast.14, f32[16,128]{1,0:T(8,128)S(1)} %bitcast.15), custom_call_target="tpu_custom_call" | custom-call | tf_op jit(solution)/shard_map/ends/pallas_call | solution.py:258
  17.2 5.5 %full.1 = bf16[3,128,32,128]{3,2,1,0:T(8,128)(2,1)} custom-call(f32[3,2048]{1,0:T(4,128)S(1)} %copy-done.1, bf16[3,128,32,128]{3,2,1,0:T(8,128)(2,1)S(1)} %bitcast.13, f32[3,16,128]{2,1,0:T(8,128)S(1)} %get-tuple-element.7.coef, f32[4,2,3,4,128]{4,3,2,1,0:T(4,128)S(1)} %get-tuple-element.8.start), custom_call_target="tpu_custom_call" | custom-call | tf_op jit(solution)/shard_map/full/pallas_call | solution.py:283
Async XLA Ops:
  0.0 1.9 %copy-start = (bf16[3,128,2,2048]{3,2,1,0:T(2,128)(2,1)S(1)}, bf16[3,128,2,2048]{3,2,1,0:T(2,128)(2,1)}, u32[]{:S(2)}) copy-start(bf16[3,128,2,2048]{3,2,1,0:T(2,128)(2,1)} %param.4) | copy-start | bytes 9437188
  1.9 0.8 %copy-start.1 = (f32[3,2048]{1,0:T(4,128)S(1)}, f32[3,2048]{1,0:T(4,128)}, u32[]{:S(2)}) copy-start(f32[3,2048]{1,0:T(4,128)} %keep.3) | copy-start | bytes 73732
  2.6 0.7 %copy-start.2 = (f32[2048]{0:T(1024)S(1)}, f32[2048]{0:T(1024)}, u32[]{:S(2)}) copy-start(f32[2048]{0:T(1024)} %param.5) | copy-start | bytes 24580
  3.3 0.7 %copy-start.3 = (f32[2048]{0:T(1024)S(1)}, f32[2048]{0:T(1024)}, u32[]{:S(2)}) copy-start(f32[2048]{0:T(1024)} %param.6) | copy-start | bytes 24580

commit v4 on v3

--- a/solution.py
+++ b/solution.py
@@ -60,7 +60,7 @@
     return a[0] * b[0] - a[1] * b[1], a[0] * b[1] + a[1] * b[0]
 
 
-def exchange(length, group, blocks, keep_rows, coef, prods, span, own, near, total, far, spread, back, sems, carry):
+def exchange(length, group, blocks, keep_rows, coef, prods, span, own, near, total, far, spread, back, sems, carry, fill_a, fill_b):
     send_a, recv_a, send_b, recv_b, send_c, recv_c = sems
     batch = own.shape[2]
     me = lax.axis_index("seq")
@@ -105,6 +105,7 @@
         logs = jnp.log(keep_rows[:, b * length : (b + 1) * length])
         prods[b] = jnp.broadcast_to(jnp.exp(jnp.sum(logs, axis=1, keepdims=True)), prods.shape[1:])
     lam = (span[part, 0], span[part, 1])
+    fill_a()
     powers = [None, lam]
     for _ in range(group - 1):
         powers.append(cmul(powers[-1], lam))
@@ -141,6 +142,7 @@
             else:
                 spread[slot, 0, s], spread[slot, 1, s] = inner[m][s]
     far[0] = jnp.zeros(far.shape[1:], jnp.float32)
+    fill_b()
     for d in range(groups - 1, 0, -1):
 
         @pl.when(at - d >= 0)
@@ -180,61 +182,114 @@
             copy_b(d).wait_send()
 
 
-def end_kernel(length, group, blocks, keep, keep_rows, x, decay, phase, carry, coef, flat, held, prods, span, own, near, total, far, spread, back, *sems):
-    step = pl.program_id(0)
-    batch, steps = x.shape[:2]
+def end_kernel(length, group, blocks, steps, keep_hbm, x_hbm, decay_hbm, phase_hbm, states, table, entry,
+               x, keep, keep_rows, decay, phase, coef, twice, prods, span, own, near, total, far, spread, back, carry,
+               x_sem, small_sem, *sems):
+    batch = states.shape[0]
+    rows = coef.shape[1]
+    chunks = length // steps
+    even = pl.ds(0, rows, stride=2)
+    odd = pl.ds(1, rows, stride=2)
+    small = [
+        pltpu.make_async_copy(src, dst, small_sem.at[i])
+        for i, (src, dst) in enumerate(
+            ((decay_hbm, decay), (phase_hbm, phase), (keep_hbm, keep), (keep_hbm, keep_rows))
+        )
+    ]
+
+    def load(i):
+        at = pl.ds(i * steps, steps)
+        return pltpu.make_async_copy(x_hbm.at[:, at], x.at[:, at], x_sem.at[i])
+
+    for copy in small[:3]:
+        copy.start()
+    for i in range(chunks):
+        load(i).start()
+    small[3].start()
+
     me = lax.axis_index("seq")
     barrier = pltpu.get_barrier_semaphore()
-    peers = group - 1 + blocks // group - 1
-
-    @pl.when(step == 0)
-    def _():
-        held[...] = jnp.zeros_like(held)
-        coef[0], coef[1], coef[2] = coefficients(decay[...], phase[...])
-        first = me // group * group
-        for d in range(1, group):
-            peer = first + lax.rem(me + d, group)
-            pl.semaphore_signal(barrier, inc=1, device_id={"seq": peer}, device_id_type=pl.DeviceIdType.MESH)
-        for d in range(1, blocks // group):
-            peer = lax.rem(me + d * group, blocks)
-            pl.semaphore_signal(barrier, inc=1, device_id={"seq": peer}, device_id_type=pl.DeviceIdType.MESH)
-
-    flat[...] = x[...].astype(jnp.float32)
-    base = me * length + step * steps
-    state = [(held[0, s], held[1, s]) for s in range(batch)]
-    state = scan_chunk(keep, base, flat, coef[0], coef[1], None, state, False)
+    first = me // group * group
+    for d in range(1, group):
+        peer = first + lax.rem(me + d, group)
+        pl.semaphore_signal(barrier, inc=1, device_id={"seq": peer}, device_id_type=pl.DeviceIdType.MESH)
+    for d in range(1, blocks // group):
+        peer = lax.rem(me + d * group, blocks)
+        pl.semaphore_signal(barrier, inc=1, device_id={"seq": peer}, device_id_type=pl.DeviceIdType.MESH)
+
+    small[0].wait()
+    small[1].wait()
+    coef[0], coef[1], coef[2] = coefficients(decay[...], phase[...])
+    for c in range(2):
+        twice[c, even, :] = coef[c]
+        twice[c, odd, :] = coef[c]
+    small[2].wait()
+    base = me * length
+    zero = jnp.zeros((rows, LANES), jnp.float32)
+    start = tuple((zero, zero) for _ in range(batch))
+
+    def ends(i, state):
+        at = pl.ds(i * steps, steps)
+        load(i).wait()
+        states[:, at] = x[:, at].astype(jnp.float32)
+        state = scan_chunk(keep, base + i * steps, states.at[:, at], coef[0], coef[1], None, list(state), False)
+        return tuple(state)
+
+    state = lax.fori_loop(0, chunks, ends, start)
+    part_rows = own.shape[3]
     for s in range(batch):
-        held[0, s], held[1, s] = state[s]
-
-    @pl.when(step == pl.num_programs(0) - 1)
-    def _():
-        part_rows = own.shape[3]
-        for s in range(batch):
-            for c in range(2):
-                value = state[s][c] * coef[2]
-                for p in range(group):
-                    own[p, c, s] = value[p * part_rows : (p + 1) * part_rows]
-        pl.semaphore_wait(barrier, peers)
-        exchange(length, group, blocks, keep_rows, coef, prods, span, own, near, total, far, spread, back, sems, carry)
-
-
-def full_kernel(length, keep, x, coef, start, out, flat, held):
-    step = pl.program_id(0)
-    batch, steps = x.shape[:2]
-
-    @pl.when(step == 0)
-    def _():
-        group, _, _, part_rows, _ = start.shape
+        for c in range(2):
+            value = state[s][c] * coef[2]
+            for p in range(group):
+                own[p, c, s] = value[p * part_rows : (p + 1) * part_rows]
+
+    def fill_a():
+        ones = jnp.ones((2 * rows, LANES), jnp.float32)
+
+        def powers(i, held):
+            power, scale = held
+            scale = list(scale)
+            for t in range(4):
+                power = cmul((twice[0], twice[1]), power)
+                for s in range(batch):
+                    scale[s] = scale[s] * keep[s, base + i * 4 + t]
+                    table[s, i * 4 + t, 0] = scale[s] * power[0]
+                    table[s, i * 4 + t, 1] = scale[s] * power[1]
+            return power, tuple(scale)
+
+        unit = tuple(jnp.float32(1) for _ in range(batch))
+        lax.fori_loop(0, length // 4, powers, ((ones, jnp.zeros_like(ones)), unit))
+
+    def fill_b():
+        def local(i, state):
+            at = pl.ds(i * steps, steps)
+            view = states.at[:, at]
+            return tuple(scan_chunk(keep, base + i * steps, view, coef[0], coef[1], coef[2], list(state), True))
+
+        lax.fori_loop(0, chunks, local, start)
+
+    small[3].wait()
+    pl.semaphore_wait(barrier, group - 1 + blocks // group - 1)
+    exchange(length, group, blocks, keep_rows, coef, prods, span, own, near, total, far, spread, back, sems, carry,
+             fill_a, fill_b)
+    for s in range(batch):
         for p in range(group):
-            held[:, :, p * part_rows : (p + 1) * part_rows] = start[p]
-
-    flat[...] = x[...].astype(jnp.float32)
-    base = lax.axis_index("seq") * length + step * steps
-    state = [(held[0, s], held[1, s]) for s in range(batch)]
-    state = scan_chunk(keep, base, flat, coef[0], coef[1], coef[2], state, True)
+            top = pl.ds(2 * p * part_rows, part_rows, stride=2)
+            low = pl.ds(2 * p * part_rows + 1, part_rows, stride=2)
+            entry[s, 0, top, :] = carry[p, 0, s]
+            entry[s, 0, low, :] = carry[p, 1, s]
+            entry[s, 1, top, :] = -carry[p, 1, s]
+            entry[s, 1, low, :] = carry[p, 0, s]
+
+
+def full_kernel(states, table, entry, out):
+    batch, steps = out.shape[:2]
+    base = pl.program_id(0) * steps
     for s in range(batch):
-        held[0, s], held[1, s] = state[s]
-    out[...] = flat[...].astype(jnp.bfloat16)
+        for t in range(steps):
+            at = base + t
+            moved = table[s, at, 0] * entry[s, 0] + table[s, at, 1] * entry[s, 1]
+            out[s, t] = (states[s, at] + moved).astype(jnp.bfloat16)
 
 
 def shards(inputs, decay_rate, phase, keep):
@@ -242,54 +297,56 @@
     rows = width // LANES
     x = split_view(inputs)
     steps = min(16, length)
-    grid = (length // steps,)
-    whole = pl.BlockSpec(memory_space=pltpu.VMEM)
-    smem = pl.BlockSpec(memory_space=pltpu.SMEM)
-    block = pl.BlockSpec((batch, steps, 2 * rows, LANES), lambda i: (0, i, 0, 0))
-    scratch = [
-        pltpu.VMEM((batch, steps, 2 * rows, LANES), jnp.float32),
-        pltpu.VMEM((2, batch, rows, LANES), jnp.float32),
-    ]
+    chunks = length // steps
     blocks = lax.axis_size("seq")
     group = 4
     groups = blocks // group
+    whole = pl.BlockSpec(memory_space=pltpu.VMEM)
+    away = pl.BlockSpec(memory_space=pltpu.HBM)
     piece = (2, batch, rows // group, LANES)
     dma = pltpu.SemaphoreType.DMA
-    carry, coef = pl.pallas_call(
-        functools.partial(end_kernel, length, group, blocks),
-        grid=grid,
+    f32 = jnp.float32
+    states, table, entry = pl.pallas_call(
+        functools.partial(end_kernel, length, group, blocks, steps),
         out_shape=(
-            jax.ShapeDtypeStruct((group,) + piece, jnp.float32),
-            jax.ShapeDtypeStruct((3, rows, LANES), jnp.float32),
+            jax.ShapeDtypeStruct((batch, length, 2 * rows, LANES), f32),
+            jax.ShapeDtypeStruct((batch, length, 2, 2 * rows, LANES), f32),
+            jax.ShapeDtypeStruct((batch, 2, 2 * rows, LANES), f32),
         ),
-        in_specs=[smem, whole, block, whole, whole],
-        out_specs=(whole, whole),
-        scratch_shapes=scratch
-        + [
-            pltpu.VMEM((blocks, batch, LANES), jnp.float32),
-            pltpu.VMEM((group, 2, rows // group, LANES), jnp.float32),
-            pltpu.VMEM((group,) + piece, jnp.float32),
-            pltpu.VMEM((group,) + piece, jnp.float32),
-            pltpu.VMEM(piece, jnp.float32),
-            pltpu.VMEM((groups,) + piece, jnp.float32),
-            pltpu.VMEM((group,) + piece, jnp.float32),
-            pltpu.VMEM((group,) + piece, jnp.float32),
+        in_specs=[away] * 4,
+        out_specs=(whole,) * 3,
+        scratch_shapes=[
+            pltpu.VMEM((batch, length, 2 * rows, LANES), jnp.bfloat16),
+            pltpu.SMEM(keep.shape, f32),
+            pltpu.VMEM(keep.shape, f32),
+            pltpu.VMEM((rows, LANES), f32),
+            pltpu.VMEM((rows, LANES), f32),
+            pltpu.VMEM((3, rows, LANES), f32),
+            pltpu.VMEM((2, 2 * rows, LANES), f32),
+            pltpu.VMEM((blocks, batch, LANES), f32),
+            pltpu.VMEM((group, 2, rows // group, LANES), f32),
+            pltpu.VMEM((group,) + piece, f32),
+            pltpu.VMEM((group,) + piece, f32),
+            pltpu.VMEM(piece, f32),
+            pltpu.VMEM((groups,) + piece, f32),
+            pltpu.VMEM((group,) + piece, f32),
+            pltpu.VMEM((group,) + piece, f32),
+            pltpu.VMEM((group,) + piece, f32),
+            dma((chunks,)), dma((4,)),
             dma((group,)), dma((group,)), dma((groups,)), dma((groups,)), dma((group,)), dma((group,)),
         ],
         compiler_params=pltpu.CompilerParams(collective_id=0, has_side_effects=True, vmem_limit_bytes=GRANT),
         name="ends",
-    )(keep, keep, x, decay_rate.reshape(rows, LANES), phase.reshape(rows, LANES))
-
+    )(keep, x, decay_rate.reshape(rows, LANES), phase.reshape(rows, LANES))
     out = pl.pallas_call(
-        functools.partial(full_kernel, length),
-        grid=grid,
+        full_kernel,
+        grid=(chunks,),
         out_shape=jax.ShapeDtypeStruct((batch, length, 2 * rows, LANES), jnp.bfloat16),
-        in_specs=[smem, block, whole, whole],
-        out_specs=block,
-        scratch_shapes=scratch,
+        in_specs=[whole] * 3,
+        out_specs=pl.BlockSpec((batch, steps, 2 * rows, LANES), lambda i: (0, i, 0, 0)),
         compiler_params=pltpu.CompilerParams(vmem_limit_bytes=GRANT),
         name="full",
-    )(keep, x, coef, carry)
+    )(states, table, entry)
     return join_view(out)
 
 

time: 23 us -> 21 us (0.913)
  the two profiles are of different devices: /device:TPU:12 before, /device:TPU:0 now
where the time goes in v4:
time: 21 us; the launch traced here: 20.7 us
  Pallas kernels  16.7 us (80%)
  local copies, waits for them, and re-layouts  4.04 us (19%)
    pallas_call x1, Pallas kernels, shards(): pl.pallas_call(functools.partial(end_kernel, length, group, blocks, steps...  13.1 us
    unnamed x8, local copies, waits for them, and re-layouts  4.04 us
    pallas_call x1, Pallas kernels, shards(): pl.pallas_call(full_kernel, grid=(chunks,), out_shape=jax.ShapeDtypeStruc...  3.62 us

profile of v4, /device:TPU:0, one launch (start us, length us, event | category | flops | bytes accessed | tf_op | source)
XLA Modules:
  0.0 20.7 jit_solution(5773421405803879601)
XLA Ops:
  0.0 0.0 copy-start
  0.0 1.9 %copy-done = bf16[3,128,2,2048]{3,2,1,0:T(2,128)(2,1)S(1)} copy-done((bf16[3,128,2,2048]{3,2,1,0:T(2,128)(2,1)S(1)}, bf16[3,128,2,2048]{3,2,1,0:T(2,128)(2,1)}, u32[]{:S(2)}) %copy-start) | copy-done | bytes 3145752
  1.9 0.0 copy-start.1
  1.9 0.8 %copy-done.1 = f32[3,2048]{1,0:T(4,128)S(1)} copy-done((f32[3,2048]{1,0:T(4,128)S(1)}, f32[3,2048]{1,0:T(4,128)}, u32[]{:S(2)}) %copy-start.1) | copy-done | bytes 24600
  2.6 0.0 copy-start.2
  2.7 0.7 %copy-done.2 = f32[2048]{0:T(1024)S(1)} copy-done((f32[2048]{0:T(1024)S(1)}, f32[2048]{0:T(1024)}, u32[]{:S(2)}) %copy-start.2) | copy-done | bytes 8216
  3.3 0.0 copy-start.3
  3.3 0.7 %copy-done.3 = f32[2048]{0:T(1024)S(1)} copy-done((f32[2048]{0:T(1024)S(1)}, f32[2048]{0:T(1024)}, u32[]{:S(2)}) %copy-start.3) | copy-done | bytes 8216
  4.0 13.1 %ends.1 = (f32[3,128,32,128]{3,2,1,0:T(8,128)S(1)}, f32[3,128,2,32,128]{4,3,2,1,0:T(8,128)S(1)}, f32[3,2,32,128]{3,2,1,0:T(8,128)S(1)}) custom-call(f32[3,2048]{1,0:T(4,128)S(1)} %copy-done.1, bf16[3,128,32,128]{3,2,1,0:T(8,128)(2,1)S(1)} %bitcast.12, f32[16,128]{1,0:T(8,128)S(1)} %bitcast.13, f32[16,128]{1,0:T(8,128)S(1)} %bitcast.14), custom_call_target="tpu_custom_call" | custom-call | tf_op jit(solution)/shard_map/ends/pallas_call | solution.py:309
  17.1 3.6 %full.1 = bf16[3,128,32,128]{3,2,1,0:T(8,128)(2,1)} custom-call(f32[3,128,32,128]{3,2,1,0:T(8,128)S(1)} %get-tuple-element.8.states, f32[3,128,2,32,128]{4,3,2,1,0:T(8,128)S(1)} %get-tuple-element.9.table, f32[3,2,32,128]{3,2,1,0:T(8,128)S(1)} %get-tuple-element.10.entry), custom_call_target="tpu_custom_call" | custom-call | tf_op jit(solution)/shard_map/full/pallas_call | solution.py:341
Async XLA Ops:
  0.0 1.9 %copy-start = (bf16[3,128,2,2048]{3,2,1,0:T(2,128)(2,1)S(1)}, bf16[3,128,2,2048]{3,2,1,0:T(2,128)(2,1)}, u32[]{:S(2)}) copy-start(bf16[3,128,2,2048]{3,2,1,0:T(2,128)(2,1)} %param.4) | copy-start | bytes 9437188
  1.9 0.8 %copy-start.1 = (f32[3,2048]{1,0:T(4,128)S(1)}, f32[3,2048]{1,0:T(4,128)}, u32[]{:S(2)}) copy-start(f32[3,2048]{1,0:T(4,128)} %keep_hbm.1) | copy-start | bytes 73732
  2.6 0.7 %copy-start.2 = (f32[2048]{0:T(1024)S(1)}, f32[2048]{0:T(1024)}, u32[]{:S(2)}) copy-start(f32[2048]{0:T(1024)} %param.5) | copy-start | bytes 24580
  3.3 0.7 %copy-start.3 = (f32[2048]{0:T(1024)S(1)}, f32[2048]{0:T(1024)}, u32[]{:S(2)}) copy-start(f32[2048]{0:T(1024)} %param.6) | copy-start | bytes 24580

commit v5 on v4

--- a/solution.py
+++ b/solution.py
@@ -182,9 +182,9 @@
             copy_b(d).wait_send()
 
 
-def end_kernel(length, group, blocks, steps, keep_hbm, x_hbm, decay_hbm, phase_hbm, states, table, entry,
-               x, keep, keep_rows, decay, phase, coef, twice, prods, span, own, near, total, far, spread, back, carry,
-               x_sem, small_sem, *sems):
+def end_kernel(length, group, blocks, steps, keep_hbm, x, decay_hbm, phase_hbm, states, table, entry,
+               keep, keep_rows, decay, phase, coef, twice, prods, span, own, near, total, far, spread, back, carry,
+               small_sem, *sems):
     batch = states.shape[0]
     rows = coef.shape[1]
     chunks = length // steps
@@ -197,15 +197,8 @@
         )
     ]
 
-    def load(i):
-        at = pl.ds(i * steps, steps)
-        return pltpu.make_async_copy(x_hbm.at[:, at], x.at[:, at], x_sem.at[i])
-
-    for copy in small[:3]:
+    for copy in small:
         copy.start()
-    for i in range(chunks):
-        load(i).start()
-    small[3].start()
 
     me = lax.axis_index("seq")
     barrier = pltpu.get_barrier_semaphore()
@@ -230,7 +223,6 @@
 
     def ends(i, state):
         at = pl.ds(i * steps, steps)
-        load(i).wait()
         states[:, at] = x[:, at].astype(jnp.float32)
         state = scan_chunk(keep, base + i * steps, states.at[:, at], coef[0], coef[1], None, list(state), False)
         return tuple(state)
@@ -313,10 +305,9 @@
             jax.ShapeDtypeStruct((batch, length, 2, 2 * rows, LANES), f32),
             jax.ShapeDtypeStruct((batch, 2, 2 * rows, LANES), f32),
         ),
-        in_specs=[away] * 4,
+        in_specs=[away, whole, away, away],
         out_specs=(whole,) * 3,
         scratch_shapes=[
-            pltpu.VMEM((batch, length, 2 * rows, LANES), jnp.bfloat16),
             pltpu.SMEM(keep.shape, f32),
             pltpu.VMEM(keep.shape, f32),
             pltpu.VMEM((rows, LANES), f32),
@@ -332,7 +323,7 @@
             pltpu.VMEM((group,) + piece, f32),
             pltpu.VMEM((group,) + piece, f32),
             pltpu.VMEM((group,) + piece, f32),
-            dma((chunks,)), dma((4,)),
+            dma((4,)),
             dma((group,)), dma((group,)), dma((groups,)), dma((groups,)), dma((group,)), dma((group,)),
         ],
         compiler_params=pltpu.CompilerParams(collective_id=0, has_side_effects=True, vmem_limit_bytes=GRANT),

time: 21 us -> 20.4 us (0.971)
  Pallas kernels: 16.7 us -> 16.1 us
    pallas_call x1, Pallas kernels: 13.1 us -> 12.5 us  [shards(): pl.pallas_call(functools.partial(end_kernel, length, group, blocks, steps...]
where the time goes in v5:
time: 20.4 us; the launch traced here: 20.2 us
  Pallas kernels  16.1 us (79%)
  local copies, waits for them, and re-layouts  4.04 us (20%)
    pallas_call x1, Pallas kernels, shards(): pl.pallas_call(functools.partial(end_kernel, length, group, blocks, steps...  12.5 us
    unnamed x8, local copies, waits for them, and re-layouts  4.04 us
    pallas_call x1, Pallas kernels, shards(): pl.pallas_call(full_kernel, grid=(chunks,), out_shape=jax.ShapeDtypeStruc...  3.62 us

profile of v5, /device:TPU:0, one launch (start us, length us, event | category | flops | bytes accessed | tf_op | source)
XLA Modules:
  0.0 20.2 jit_solution(16327659202889352985)
XLA Ops:
  0.0 0.0 copy-start
  0.0 1.9 %copy-done = bf16[3,128,2,2048]{3,2,1,0:T(2,128)(2,1)S(1)} copy-done((bf16[3,128,2,2048]{3,2,1,0:T(2,128)(2,1)S(1)}, bf16[3,128,2,2048]{3,2,1,0:T(2,128)(2,1)}, u32[]{:S(2)}) %copy-start) | copy-done | bytes 3145752
  1.9 0.0 copy-start.1
  1.9 0.8 %copy-done.1 = f32[3,2048]{1,0:T(4,128)S(1)} copy-done((f32[3,2048]{1,0:T(4,128)S(1)}, f32[3,2048]{1,0:T(4,128)}, u32[]{:S(2)}) %copy-start.1) | copy-done | bytes 24600
  2.6 0.0 copy-start.2
  2.7 0.7 %copy-done.2 = f32[2048]{0:T(1024)S(1)} copy-done((f32[2048]{0:T(1024)S(1)}, f32[2048]{0:T(1024)}, u32[]{:S(2)}) %copy-start.2) | copy-done | bytes 8216
  3.3 0.0 copy-start.3
  3.3 0.7 %copy-done.3 = f32[2048]{0:T(1024)S(1)} copy-done((f32[2048]{0:T(1024)S(1)}, f32[2048]{0:T(1024)}, u32[]{:S(2)}) %copy-start.3) | copy-done | bytes 8216
  4.0 12.5 %ends.1 = (f32[3,128,32,128]{3,2,1,0:T(8,128)S(1)}, f32[3,128,2,32,128]{4,3,2,1,0:T(8,128)S(1)}, f32[3,2,32,128]{3,2,1,0:T(8,128)S(1)}) custom-call(f32[3,2048]{1,0:T(4,128)S(1)} %copy-done.1, bf16[3,128,32,128]{3,2,1,0:T(8,128)(2,1)S(1)} %bitcast.12, f32[16,128]{1,0:T(8,128)S(1)} %bitcast.13, f32[16,128]{1,0:T(8,128)S(1)} %bitcast.14), custom_call_target="tpu_custom_call" | custom-call | tf_op jit(solution)/shard_map/ends/pallas_call | solution.py:301
  16.5 3.6 %full.1 = bf16[3,128,32,128]{3,2,1,0:T(8,128)(2,1)} custom-call(f32[3,128,32,128]{3,2,1,0:T(8,128)S(1)} %get-tuple-element.8.states, f32[3,128,2,32,128]{4,3,2,1,0:T(8,128)S(1)} %get-tuple-element.9.table, f32[3,2,32,128]{3,2,1,0:T(8,128)S(1)} %get-tuple-element.10.entry), custom_call_target="tpu_custom_call" | custom-call | tf_op jit(solution)/shard_map/full/pallas_call | solution.py:332
Async XLA Ops:
  0.0 1.9 %copy-start = (bf16[3,128,2,2048]{3,2,1,0:T(2,128)(2,1)S(1)}, bf16[3,128,2,2048]{3,2,1,0:T(2,128)(2,1)}, u32[]{:S(2)}) copy-start(bf16[3,128,2,2048]{3,2,1,0:T(2,128)(2,1)} %param.4) | copy-start | bytes 9437188
  1.9 0.8 %copy-start.1 = (f32[3,2048]{1,0:T(4,128)S(1)}, f32[3,2048]{1,0:T(4,128)}, u32[]{:S(2)}) copy-start(f32[3,2048]{1,0:T(4,128)} %keep_hbm.1) | copy-start | bytes 73732
  2.6 0.7 %copy-start.2 = (f32[2048]{0:T(1024)S(1)}, f32[2048]{0:T(1024)}, u32[]{:S(2)}) copy-start(f32[2048]{0:T(1024)} %param.5) | copy-start | bytes 24580
  3.3 0.7 %copy-start.3 = (f32[2048]{0:T(1024)S(1)}, f32[2048]{0:T(1024)}, u32[]{:S(2)}) copy-start(f32[2048]{0:T(1024)} %param.6) | copy-start | bytes 24580
